TPU v7x, 8 devices: a whole 2x2x1 slice. The times are simulated.
8 devices in a mesh: dp: 1 (over z), tp: 8 (over x, y, core).
Axes of the slice: x: 2, y: 2, z: 1, core: 2. Of those that a mesh axis runs over, the one named last changes fastest.
Arguments:
- x: bfloat16 [2048, 5120], P('dp')
- w_gate: bfloat16 [5120, 32768], P(None, 'tp')
- w_up: bfloat16 [5120, 32768], P(None, 'tp')
- w_down: bfloat16 [32768, 5120], P('tp')
Outputs:
- output: bfloat16 [2048, 5120], P('dp')
All inputs are finite; a program needn't handle non-finite values.
Results may differ from a plain program's by a relative error of at most 0.016.
Values are sent between devices in bfloat16 or wider.
A program may use at most 2 GiB of HBM per device.

v0:
```python
import jax
import jax.numpy as jnp
from jax import lax
from jax.sharding import PartitionSpec as P


def solution(mesh):
    def step(x, w_gate, w_up, w_down):
        gate = jnp.dot(x, w_gate, preferred_element_type=jnp.float32)
        up = jnp.dot(x, w_up, preferred_element_type=jnp.float32)
        hidden = (jax.nn.silu(gate) * up).astype(jnp.bfloat16)
        term = jnp.dot(hidden, w_down, preferred_element_type=jnp.float32).astype(jnp.bfloat16)
        return lax.psum(term, "tp")

    return jax.shard_map(
        step,
        mesh=mesh,
        in_specs=(P("dp", None), P(None, "tp"), P(None, "tp"), P("tp", None)),
        out_specs=P("dp", None),
        check_vma=False,
    )
```

profile of v0, /device:TPU:0, one launch (start us, length us, event | category | flops | bytes accessed | tf_op | source)
XLA Modules:
  0.0 583.1 jit_solution(2895081801580078242)
XLA Ops:
  6.5 0.0 all-reduce.2.cloned.1.call-start
  6.5 96.8 %fusion = f32[2048,4096]{1,0:T(8,128)} fusion(bf16[2048,5120]{1,0:T(8,128)(2,1)} %param.4, bf16[5120,4096]{1,0:T(8,128)(2,1)} %param.5), kind=kOutput, calls=%fused_computation.2 | convolution fusion | flops 85899345920 | bytes 96468992 | tf_op jit(solution)/shard_map/dot_general | solution.py:9
  103.3 105.4 %multiply_convert_fusion = bf16[2048,4096]{1,0:T(8,128)(2,1)} fusion(f32[2048,4096]{1,0:T(8,128)} %fusion, bf16[2048,5120]{1,0:T(8,128)(2,1)} %param.4, bf16[5120,4096]{1,0:T(8,128)(2,1)} %param.6), kind=kOutput, calls=%fused_computation | convolution fusion | flops 85949677568 | bytes 113246208 | tf_op jit(solution)/shard_map/dot_general | solution.py:10
  208.7 95.9 %convolution_convert_fusion = bf16[2048,5120]{1,0:T(8,128)(2,1)} fusion(bf16[2048,4096]{1,0:T(8,128)(2,1)} %multiply_convert_fusion, bf16[4096,5120]{1,0:T(8,128)(2,1)} %param.7), kind=kOutput, calls=%fused_computation.1 | convolution fusion | flops 85909831680 | bytes 79691776 | tf_op jit(solution)/shard_map/dot_general | solution.py:12
  304.5 0.0 all-reduce.2.cloned.1.call-update
  304.6 254.3 %all-reduce.2.cloned.1.call-done = bf16[2048,5120]{1,0:T(8,128)(2,1)} async-done(((bf16[2048,5120]{1,0:T(8,128)(2,1)}), bf16[2048,5120]{1,0:T(8,128)(2,1)}) %all-reduce.2.cloned.1.call-update) | async-done | bytes 20971536 | tf_op jit(solution)/shard_map/psum | solution.py:13
  558.9 17.3 %copy.6 = bf16[2048,5120]{1,0:T(8,128)(2,1)} copy(bf16[2048,5120]{1,0:T(8,128)(2,1)} %all-reduce.2.cloned.1.call-done) | data formatting | bytes 41943040
Async XLA Ops:
  6.5 552.4 %all-reduce.2.cloned.1.call-start = ((), (), s32[]{:S(2)}) async-start(), calls=%async_computation | async-start | bytes 41943040 | tf_op jit(solution)/shard_map/psum | solution.py:13
Sparse Core Ops, SparseCore 0:
  304.7 254.1 all-reduce.1
where the time goes:
time: 583 us
  matrix products  298 us (51%)
  waiting for transfers between devices  254 us (44%)
  local copies, waits for them, and re-layouts  17.3 us (3%)
  between operations  13.4 us (2%)
    psum x1, waiting for transfers between devices, step(): return lax.psum(term, 'tp')  254 us
    dot_general x1, matrix products, step(): up = jnp.dot(x, w_up, preferred_element_type=jnp.float32)  105 us
    dot_general x1, matrix products, step(): gate = jnp.dot(x, w_gate, preferred_element_type=jnp.float32)  96.8 us
    dot_general x1, matrix products, step(): jnp.dot(hidden, w_down, preferred_element_type=jnp.float32)  95.9 us
    unnamed x1, local copies, waits for them, and re-layouts  17.3 us
  transfers between devices with their start and end apart: 1, of which 1 were waited for; matrix products, arithmetic and copies ran while one was open for 0% of the time, Pallas kernels for 0%

commit v1 on v0

v1 whole, which is shorter than its diff:
```python
import functools

import jax
import jax.numpy as jnp
from jax import lax
from jax.experimental import pallas as pl
from jax.experimental.pallas import tpu as pltpu
from jax.sharding import PartitionSpec as P

MESH = pl.DeviceIdType.MESH
CHUNKS = (512, 512, 512, 512)
TF = 256
TD = 512
SLOTS = 3
AHEAD = SLOTS - 1
F32, BF16 = jnp.float32, jnp.bfloat16

STRIDE = 2
LAGS = (1, 3, 5, 7, 9, 11)
COMM = True


def al(i, m=16):
    return pl.multiple_of(i, m)


def kernel(x_hbm, wg_hbm, wu_hbm, wd_hbm, y_hbm, xbuf, h, w, own, send_a, recv_a, send_b, recv_b,
           send_c, recv_c, fin, wsem, xsem, ssem, rsem):
    depth, ff = wg_hbm.shape
    n_g, n_d = ff // TF, depth // TD
    period = n_g + n_d

    tp = lax.axis_index("tp")
    core = tp % 2
    yb = (tp // 2) % 2
    xb = tp // 4
    partner = tp + 1 - 2 * core
    xn = tp + 4 - 8 * xb
    yn = tp + 2 - 4 * yb
    n1 = xn + core * (yn - xn)
    n2 = yn + core * (xn - yn)
    p1 = xb + core * (yb - xb)
    p2 = yb + core * (xb - yb)

    if COMM:
        barrier = pltpu.get_barrier_semaphore()
        for dev in (partner, xn, yn):
            pl.semaphore_signal(barrier, inc=1, device_id={"tp": dev}, device_id_type=MESH)
        pl.semaphore_wait(barrier, 3)

    def weights(slot, t, gate_up):
        if gate_up:
            cols = pl.ds(al(t * TF, TF), TF)
            return (pltpu.make_async_copy(wg_hbm.at[:, cols], w.at[slot, :, pl.ds(0, TF)], wsem.at[slot, 0]),
                    pltpu.make_async_copy(wu_hbm.at[:, cols], w.at[slot, :, pl.ds(TF, TF)], wsem.at[slot, 1]))
        cols = pl.ds(al(t * TD, TD), TD)
        return (pltpu.make_async_copy(wd_hbm.at[:, cols], w.at[slot, pl.ds(0, ff), pl.ds(0, TD)], wsem.at[slot, 0]),)

    def issue(slot, t, gate_up):
        for copy in weights(slot, t, gate_up):
            copy.start()

    def x_copy(r0, rows):
        return pltpu.make_async_copy(x_hbm.at[pl.ds(r0, rows)], xbuf.at[pl.ds(0, rows)], xsem)

    def remote(src, dst, j, s, r, dev):
        return pltpu.make_async_remote_copy(
            src_ref=src, dst_ref=dst, send_sem=ssem.at[j, s], recv_sem=rsem.at[j, r],
            device_id={"tp": dev}, device_id_type=MESH)

    def copies(r0, rows, j):
        half, quarter, eighth = rows // 2, rows // 4, rows // 8
        cols = pl.ds(al(j * TD, TD), TD)

        def y_at(off, n):
            return y_hbm.at[pl.ds(al(off), n), cols]

        mine = r0 + core * half
        theirs = r0 + (1 - core) * half
        piece = y_at(mine + p1 * quarter + p2 * eighth, eighth)
        piece2 = y_at(mine + p1 * quarter + (1 - p2) * eighth, eighth)
        piece1 = y_at(mine + (1 - p1) * quarter + p2 * eighth, eighth)
        piece12 = y_at(mine + (1 - p1) * quarter + (1 - p2) * eighth, eighth)
        quarter1 = y_at(mine + (1 - p1) * quarter, quarter)
        their = y_at(theirs + p2 * quarter + p1 * eighth, eighth)
        their2 = y_at(theirs + p2 * quarter + (1 - p1) * eighth, eighth)
        theirq = y_at(theirs + (1 - p2) * quarter, quarter)
        f = fin.at[j, pl.ds(0, eighth)]
        sa, ra = send_a.at[j, pl.ds(0, half)], recv_a.at[j, pl.ds(0, half)]
        sb, rb = send_b.at[j, pl.ds(0, quarter)], recv_b.at[j, pl.ds(0, quarter)]
        sc, rc = send_c.at[j, pl.ds(0, eighth)], recv_c.at[j, pl.ds(0, eighth)]
        out = dict(
            a=lambda: remote(sa, ra, j, 0, 0, partner),
            b=lambda: remote(sb, rb, j, 1, 1, n1),
            c=lambda: remote(sc, rc, j, 2, 2, n2),
            local=lambda: pltpu.make_async_copy(f, piece, ssem.at[j, 3]),
            f2=lambda: remote(f, piece, j, 4, 3, n2),
            f1=lambda: remote(f, piece, j, 5, 4, n1),
            fp=lambda: remote(f, piece, j, 6, 6, partner),
            g1=lambda: remote(piece2, piece2, j, 7, 5, n1),
            gp=lambda: remote(piece2, piece2, j, 8, 7, partner),
            qp=lambda: remote(quarter1, quarter1, j, 9, 8, partner),
        )
        waits = dict(
            f2=lambda: remote(f, piece2, j, 4, 3, n2),
            f1=lambda: remote(f, piece1, j, 5, 4, n1),
            g1=lambda: remote(piece2, piece12, j, 7, 5, n1),
            fp=lambda: remote(f, their, j, 6, 6, partner),
            gp=lambda: remote(piece2, their2, j, 8, 7, partner),
            qp=lambda: remote(quarter1, theirq, j, 9, 8, partner),
        )
        return out, waits

    def stage_b(r0, rows, j):
        half, quarter, eighth = rows // 2, rows // 4, rows // 8
        c, _ = copies(r0, rows, j)
        c["a"]().wait_recv()
        go = pl.ds(al((1 - p1) * quarter), quarter)
        keep = pl.ds(al(p1 * quarter), quarter)
        send_b[j, pl.ds(0, quarter)] = (own[j, go] + recv_a[j, go].astype(F32)).astype(BF16)
        c["b"]().start()
        own[j, keep] = own[j, keep] + recv_a[j, keep].astype(F32)

    def stage_c(r0, rows, j):
        half, quarter, eighth = rows // 2, rows // 4, rows // 8
        c, _ = copies(r0, rows, j)
        c["b"]().wait_recv()
        go = pl.ds(al(p1 * quarter + (1 - p2) * eighth), eighth)
        keep = pl.ds(al(p1 * quarter + p2 * eighth), eighth)
        send_c[j, pl.ds(0, eighth)] = (
            own[j, go] + recv_b[j, pl.ds(al((1 - p2) * eighth), eighth)].astype(F32)).astype(BF16)
        c["c"]().start()
        own[j, keep] = own[j, keep] + recv_b[j, pl.ds(al(p2 * eighth), eighth)].astype(F32)

    def stage_f(r0, rows, j):
        half, quarter, eighth = rows // 2, rows // 4, rows // 8
        c, _ = copies(r0, rows, j)
        c["c"]().wait_recv()
        keep = pl.ds(al(p1 * quarter + p2 * eighth), eighth)
        fin[j, pl.ds(0, eighth)] = (own[j, keep] + recv_c[j, pl.ds(0, eighth)].astype(F32)).astype(BF16)
        c["f2"]().start()
        c["f1"]().start()
        c["fp"]().start()
        c["local"]().start()

    def stage_g(r0, rows, j):
        c, got = copies(r0, rows, j)
        got["f2"]().wait_recv()
        c["g1"]().start()
        c["gp"]().start()

    def stage_q(r0, rows, j):
        c, got = copies(r0, rows, j)
        got["f1"]().wait_recv()
        got["g1"]().wait_recv()
        c["qp"]().start()

    def stage_e(r0, rows, j):
        c, got = copies(r0, rows, j)
        for k in ("fp", "gp", "qp"):
            got[k]().wait_recv()
        c["local"]().wait()
        for k in ("a", "b", "c", "f2", "f1", "fp", "g1", "gp", "qp"):
            c[k]().wait_send()

    stages = (stage_b, stage_c, stage_f, stage_g, stage_q, stage_e)

    def tick(r0, rows, t, stride, lo=0):
        if not COMM:
            return
        for lag, stage in zip(LAGS, stages):
            u = t - lag
            j = (u + 64 * stride) // stride - 64
            due = (u >= 0) & (u < stride * n_d) & ((u + 64 * stride) % stride == 0)
            pl.when(due)(functools.partial(stage, r0, rows, j))

    n_ticks = lambda stride: LAGS[-1] + stride * (n_d - 1) + 1

    r0s = [sum(CHUNKS[:i]) for i in range(len(CHUNKS))]
    x_copy(r0s[0], CHUNKS[0]).start()
    for t in range(AHEAD):
        issue(t % SLOTS, t, True)

    for c, (r0, rows) in enumerate(zip(r0s, CHUNKS)):
        half = rows // 2
        base = c * period
        x_copy(r0, rows).wait()

        def gate_up_step(s, _, c=c, base=base, rows=rows):
            slot = (base + s) % SLOTS
            nslot = (base + s + AHEAD) % SLOTS
            nxt = s + AHEAD
            pl.when(nxt < n_g)(lambda: issue(nslot, nxt, True))
            pl.when(nxt >= n_g)(lambda: issue(nslot, nxt - n_g, False))
            if c > 0:
                tick(r0s[c - 1], CHUNKS[c - 1], n_d + s, STRIDE)
            for copy in weights(slot, s, True):
                copy.wait()
            r = jnp.dot(xbuf[pl.ds(0, rows)], w[slot], preferred_element_type=F32)
            gate, up = r[:, :TF], r[:, TF:]
            h[pl.ds(0, rows), pl.ds(al(s * TF, TF), TF)] = (gate / (1.0 + jnp.exp(-gate)) * up).astype(BF16)
            return 0

        lax.fori_loop(0, n_g, gate_up_step, 0)
        last = c == len(CHUNKS) - 1
        if not last:
            x_copy(r0s[c + 1], CHUNKS[c + 1]).start()

        def down_step(j, _, c=c, base=base, rows=rows, r0=r0, last=last):
            half = rows // 2
            slot = (base + n_g + j) % SLOTS
            nslot = (base + n_g + j + AHEAD) % SLOTS
            nxt = j + AHEAD
            pl.when(nxt < n_d)(lambda: issue(nslot, nxt, False))
            if not last:
                pl.when(nxt >= n_d)(lambda: issue(nslot, nxt - n_d, True))
            if c > 0:
                tick(r0s[c - 1], CHUNKS[c - 1], n_d + n_g + j, STRIDE)
            tick(r0, rows, j, 1 if last else STRIDE)
            for copy in weights(slot, j, False):
                copy.wait()
            wd = w[slot, pl.ds(0, ff), pl.ds(0, TD)]
            send_a[j, pl.ds(0, half)] = jnp.dot(
                h[pl.ds(al((1 - core) * half), half)], wd, preferred_element_type=F32).astype(BF16)
            if COMM:
                copies(r0, rows, j)[0]["a"]().start()
            own[j, pl.ds(0, half)] = jnp.dot(
                h[pl.ds(al(core * half), half)], wd, preferred_element_type=F32)
            return 0

        lax.fori_loop(0, n_d, down_step, 0)

    def tail(t, _):
        tick(r0s[-1], CHUNKS[-1], t, 1)
        return 0

    if COMM:
        lax.fori_loop(n_d, n_ticks(1), tail, 0)


def solution(mesh):
    def step(x, w_gate, w_up, w_down):
        depth, ff = w_gate.shape
        n_d = depth // TD
        rows = max(CHUNKS)
        hbm = pl.BlockSpec(memory_space=pl.ANY)
        y = pl.pallas_call(
            kernel,
            out_shape=jax.ShapeDtypeStruct(x.shape, x.dtype),
            in_specs=[hbm] * 4,
            out_specs=hbm,
            scratch_shapes=[
                pltpu.VMEM((rows, depth), BF16),
                pltpu.VMEM((rows, ff), BF16),
                pltpu.VMEM((SLOTS, depth, max(2 * TF, TD)), BF16),
                pltpu.VMEM((n_d, rows // 2, TD), F32),
                pltpu.VMEM((n_d, rows // 2, TD), BF16),
                pltpu.VMEM((n_d, rows // 2, TD), BF16),
                pltpu.VMEM((n_d, rows // 4, TD), BF16),
                pltpu.VMEM((n_d, rows // 4, TD), BF16),
                pltpu.VMEM((n_d, rows // 8, TD), BF16),
                pltpu.VMEM((n_d, rows // 8, TD), BF16),
                pltpu.VMEM((n_d, rows // 8, TD), BF16),
                pltpu.SemaphoreType.DMA((SLOTS, 2)),
                pltpu.SemaphoreType.DMA,
                pltpu.SemaphoreType.DMA((n_d, 10)),
                pltpu.SemaphoreType.DMA((n_d, 9)),
            ],
            compiler_params=pltpu.CompilerParams(
                collective_id=0 if COMM else None, has_side_effects=True, vmem_limit_bytes=60 * 2**20),
            name="mlp",
        )(x, w_gate, w_up, w_down)
        return y

    return jax.shard_map(
        step,
        mesh=mesh,
        in_specs=(P("dp", None), P(None, "tp"), P(None, "tp"), P("tp", None)),
        out_specs=P("dp", None),
        check_vma=False,
    )
```

time: 583 us -> 358 us (0.61)
  Pallas kernels: 0 us -> 340 us
  matrix products: 298 us -> 0 us
  waiting for transfers between devices: 254 us -> 0 us
  between operations: 13.4 us -> 0.01 us
    pallas_call x0 -> x1, Pallas kernels: none -> 340 us  [step(): pl.pallas_call(kernel, out_shape=jax.ShapeDtypeStruct(x.shape, x.dtype),...]
    dot_general x3 -> x0, matrix products: 298 us -> none  [the longest x1 105 us: step(): up = jnp.dot(x, w_up, preferred_element_type=jnp.float32)]
    psum x1 -> x0, waiting for transfers between devices: 254 us -> none  [step(): return lax.psum(term, 'tp')]
  transfers between devices with their start and end apart: 1 -> 0, of which waited for: 1 -> 0; matrix products, arithmetic and copies ran while one was open for 0% -> 0% of each run, Pallas kernels for 0% -> 0%
where the time goes in v1:
time: 358 us; the launch traced here: 357 us
  Pallas kernels  340 us (95%)
  local copies, waits for them, and re-layouts  17.3 us (5%)
    pallas_call x1, Pallas kernels, step(): pl.pallas_call(kernel, out_shape=jax.ShapeDtypeStruct(x.shape, x.dtype),...  340 us
    unnamed x1, local copies, waits for them, and re-layouts  17.3 us

profile of v1, /device:TPU:0, one launch (start us, length us, event | category | flops | bytes accessed | tf_op | source)
XLA Modules:
  0.0 357.4 jit_solution(13171601103324717140)
XLA Ops:
  0.0 340.1 %mlp.1 = bf16[2048,5120]{1,0:T(8,128)(2,1)} custom-call(bf16[2048,5120]{1,0:T(8,128)(2,1)} %x_hbm.1, bf16[5120,4096]{1,0:T(8,128)(2,1)} %wg_hbm.1, bf16[5120,4096]{1,0:T(8,128)(2,1)} %wu_hbm.1, bf16[4096,5120]{1,0:T(8,128)(2,1)} %wd_hbm.1), custom_call_target="tpu_custom_call" | custom-call | tf_op jit(solution)/shard_map/mlp/pallas_call | solution.py:247
  340.1 17.3 %copy.6 = bf16[2048,5120]{1,0:T(8,128)(2,1)} copy(bf16[2048,5120]{1,0:T(8,128)(2,1)} %mlp.1) | data formatting | bytes 41943040
